TPU v7x, 64 devices: a 2x2x8 block of a 4x4x8 slice. The times are simulated.
64 devices in a mesh: dp: 4 (over x, y), sp: 16 (over z, core).
Axes of the slice: x: 2, y: 2, z: 8, core: 2. Of those that a mesh axis runs over, the one named last changes fastest.
The devices are a block of a 4x4x8 slice.
Arguments:
- x: bfloat16 [32, 2048, 128], P('dp', 'sp'), parts along dimension 0
- w_cur: bfloat16 [16, 10, 128, 256], replicated
- w_past: bfloat16 [16, 10, 128, 256], replicated
- w_res: bfloat16 [16, 10, 128, 128], replicated
- w_skip: bfloat16 [16, 10, 128, 128], replicated
Outputs:
- output 1: float32 [32, 16, 128, 128], P('dp', 'sp'), parts along dimension 0
- output 2: float32 [32, 16, 128, 128], P('dp', 'sp'), parts along dimension 0
There are 4 independent parts. A program takes and returns all parts, laid end to end along the dimension named above; an argument that names none is the same for every part.
All inputs are finite; a program needn't handle non-finite values.
Results may differ from a plain program's by a relative error of at most 0.00880401.
Values are sent between devices in bfloat16 or wider.
A program may use at most 768 MiB of HBM per device.

v0:
```python
import functools

import jax
import jax.numpy as jnp
from jax import lax
from jax.experimental import pallas as pl
from jax.experimental.pallas import tpu as pltpu
from jax.sharding import PartitionSpec as P

F32, BF16 = jnp.float32, jnp.bfloat16
BLOCK = 256
LAG_GATE, LAG_ADD = 2, 4
GROUP = 2


def halo_slots(cycle_len):
    sizes = [max(16, 2**layer) for layer in range(cycle_len)]
    starts = [sum(sizes[:layer]) for layer in range(cycle_len)]
    return sizes, starts, sum(sizes)


def kernel(group_n, x_hbm, wc_hbm, wp_hbm, wr_hbm, ws_hbm, h_out, s_out, w_cur, w_past, w_res, w_skip, h_buf, s_buf, u_buf, halo, tail, x_in, x_all,
           h_stage, s_stage, w_sem, x_sem, x_send, x_recv, halo_send, halo_recv, out_send, out_recv):
    batch_n, seq_dev, chan = x_in.shape
    stacks, cycle_len = w_cur.shape[:2]
    rows = batch_n * seq_dev
    cores = group_n // batch_n
    pad = u_buf.shape[1] - rows
    top = h_buf.shape[0] - rows
    sizes, starts, halo_rows = halo_slots(cycle_len)
    me = lax.axis_index("sp")
    chip, core = me // cores, lax.rem(me, cores)
    far_first = sorted(range(batch_n), key=lambda off: -min(off, batch_n - off))

    x_copy = pltpu.make_async_copy(x_hbm, x_in, x_sem)
    x_copy.start()
    pairs = ((wc_hbm, w_cur), (wp_hbm, w_past), (wr_hbm, w_res), (ws_hbm, w_skip))

    def weight_copies(turn):
        part = pl.ds(turn * GROUP, GROUP)
        return [pltpu.make_async_copy(src.at[part], dst.at[part], w_sem.at[turn, k]) for k, (src, dst) in enumerate(pairs)]

    for turn in range(stacks // GROUP):
        for copy in weight_copies(turn):
            copy.start()

    barrier = pltpu.get_barrier_semaphore()
    for off in range(1, group_n):
        pl.semaphore_signal(barrier, inc=1, device_id={"sp": lax.rem(me + off, group_n)}, device_id_type=pl.DeviceIdType.MESH)

    @pl.when(core == 0)
    def _():
        halo[...] = jnp.zeros_like(halo)

    s_buf[...] = jnp.zeros_like(s_buf)
    h_buf[0:top, :] = jnp.zeros((top, chan), F32)
    pl.semaphore_wait(barrier, group_n - 1)

    half, place = me // batch_n, lax.rem(me, batch_n)
    x_copy.wait()

    def x_copies(off):
        seq = lax.rem(chip + off, batch_n)
        target = seq * cores + half
        dst = x_all.at[pl.ds(place * seq_dev, seq_dev)]

        def local():
            return pltpu.make_async_copy(x_in.at[seq], dst, x_recv.at[place])

        def remote():
            return pltpu.make_async_remote_copy(x_in.at[seq], dst, x_send.at[off], x_recv.at[place], device_id={"sp": target},
                                                device_id_type=pl.DeviceIdType.MESH)

        return target, local, remote

    for off in far_first:
        target, local, remote = x_copies(off)
        if off:
            remote().start()
        else:
            pl.when(target == me)(lambda: local().start())
            pl.when(target != me)(lambda: remote().start())
    for src in range(batch_n):
        dst = x_all.at[pl.ds(src * seq_dev, seq_dev)]
        pltpu.make_async_copy(dst, dst, x_recv.at[src]).wait()
    x = x_all[...]
    h_buf[top:, :] = x.astype(F32)
    u_buf[0, pad:, :] = x
    tail[0, starts[0]:starts[0] + sizes[0], :] = x[rows - sizes[0]:]

    def halo_copy(turn):
        part = pl.ds(turn * GROUP, GROUP)
        return pltpu.make_async_remote_copy(tail.at[part], halo.at[part], halo_send.at[turn], halo_recv.at[turn],
                                            device_id={"sp": jnp.minimum(me + 1, group_n - 1)}, device_id_type=pl.DeviceIdType.MESH)

    blocks = rows // BLOCK

    def dot(lhs, rhs):
        return jnp.dot(lhs, rhs, preferred_element_type=F32)

    def group_of_stacks(turn, carry):
        base = turn * GROUP
        for copy in weight_copies(turn):
            copy.wait()
        pl.when(core > 0)(lambda: halo_copy(turn).wait_recv())
        pre, outs = {}, {}

        def taps(step):
            layer, block = divmod(step, blocks)
            part, pos = divmod(layer, cycle_len)
            dilation = 2**pos
            if block == 0:
                got = halo[base + part, starts[pos]:starts[pos] + sizes[pos], :]
                u_buf[pos, pad - sizes[pos]:pad, :] = got
                if pos == 0:
                    h_buf[0:top, :] = got[sizes[pos] - top:].astype(F32)
            at = pad + block * BLOCK
            now = u_buf[pos, at:at + BLOCK, :]
            if dilation == 1:
                past = h_buf[top + block * BLOCK - 1:top + (block + 1) * BLOCK - 1, :].astype(BF16)
            else:
                past = u_buf[pos, at - dilation:at - dilation + BLOCK, :]
            both = jnp.concatenate([w_cur[base + part, pos], w_past[base + part, pos]], axis=0)
            pre[step] = dot(jnp.concatenate([now, past], axis=1), both)

        def gate(step):
            part, pos = divmod(step // blocks, cycle_len)
            z = pre.pop(step)
            a = (jnp.tanh(z[:, :chan]) * (0.5 * jnp.tanh(0.5 * z[:, chan:]) + 0.5)).astype(BF16)
            outs[step] = dot(a, jnp.concatenate([w_res[base + part, pos], w_skip[base + part, pos]], axis=1))

        def add(step):
            layer, block = divmod(step, blocks)
            part, pos = divmod(layer + 1, cycle_len)
            out = outs.pop(step)
            first, last = block * BLOCK, (block + 1) * BLOCK
            h = h_buf[top + first:top + last, :] + out[:, :chan]
            h_buf[top + first:top + last, :] = h
            s_buf[first:last, :] = s_buf[first:last, :] + out[:, chan:]
            u = h.astype(BF16)
            u_buf[pos, pad + first:pad + last, :] = u
            kept = max(first, rows - sizes[pos])
            if kept < last:
                at = starts[pos] + kept - (rows - sizes[pos])
                tail[base + part, at:at + last - kept, :] = u[kept - first:]

        steps = GROUP * cycle_len * blocks
        for step in range(steps + LAG_ADD):
            if step >= LAG_ADD:
                add(step - LAG_ADD)
            if LAG_GATE <= step < steps + LAG_GATE:
                gate(step - LAG_GATE)
            if step < steps:
                taps(step)
        pl.when(core < cores - 1)(lambda: halo_copy(turn).start())
        return carry

    lax.fori_loop(0, stacks // GROUP, group_of_stacks, 0)

    part_rows = rows // group_n
    spread = [(off, sub) for off in far_first for sub in range(cores)]

    def out_target(off, sub):
        return lax.rem(chip + off, batch_n) * cores + sub

    def out_copies(off, sub):
        target = out_target(off, sub)
        rank = off * cores + sub
        found = []
        for kind, (stage, out) in enumerate(((s_stage, s_out), (h_stage, h_out))):
            dst = out.at[chip, 0, pl.ds(core * part_rows, part_rows)]

            def local(kind=kind, stage=stage, dst=dst):
                return pltpu.make_async_copy(stage.at[target], dst, out_recv.at[kind, me])

            def remote(kind=kind, stage=stage, dst=dst):
                return pltpu.make_async_remote_copy(stage.at[target], dst, out_send.at[kind, rank], out_recv.at[kind, me],
                                                    device_id={"sp": target}, device_id_type=pl.DeviceIdType.MESH)

            found.append((local, remote))
        return target, found

    def send(off, sub):
        target, found = out_copies(off, sub)
        for local, remote in found:
            if off:
                remote().start()
            else:
                pl.when(target == me)(lambda: local().start())
                pl.when(target != me)(lambda: remote().start())

    for rank, (off, sub) in enumerate(spread):
        target = out_target(off, sub)
        s_stage[target] = s_buf[pl.ds(target, part_rows, stride=group_n), :]
        h_stage[target] = h_buf[pl.ds(top + target, part_rows, stride=group_n), :]
        if rank:
            send(*spread[rank - 1])
    send(*spread[-1])

    for off in range(batch_n):
        target, local, remote = x_copies(off)
        if off:
            remote().wait_send()
        else:
            pl.when(target != me)(lambda: remote().wait_send())

    def end_halo(turn, carry):
        halo_copy(turn).wait_send()
        return carry

    @pl.when(core < cores - 1)
    def _():
        lax.fori_loop(0, stacks // GROUP, end_halo, 0)

    for off, sub in spread:
        target, found = out_copies(off, sub)
        for local, remote in found:
            if off:
                remote().wait_send()
            else:
                pl.when(target != me)(lambda: remote().wait_send())
    for src in range(group_n):
        for kind, out in enumerate((s_out, h_out)):
            dst = out.at[src // cores, 0, pl.ds(src % cores * part_rows, part_rows)]
            pltpu.make_async_copy(dst, dst, out_recv.at[kind, src]).wait()


def solution(mesh):
    group_n = mesh.shape["sp"]

    def local_stack(x, w_cur, w_past, w_res, w_skip):
        batch_n, seq_dev, chan = x.shape
        stacks, cycle_len = w_cur.shape[:2]
        rows = batch_n * seq_dev
        sizes, starts, halo_rows = halo_slots(cycle_len)
        pad, top = 2 ** (cycle_len - 1), 8
        turns = stacks // GROUP
        vmem, dma = pltpu.VMEM, pltpu.SemaphoreType.DMA
        out = jax.ShapeDtypeStruct((batch_n, 1, seq_dev, chan), F32)
        hbm = pl.BlockSpec(memory_space=pltpu.HBM)
        return pl.pallas_call(
            functools.partial(kernel, group_n),
            out_shape=[out, out],
            in_specs=[hbm] * 5,
            out_specs=[hbm] * 2,
            scratch_shapes=[
                vmem(w_cur.shape, BF16), vmem(w_past.shape, BF16), vmem(w_res.shape, BF16), vmem(w_skip.shape, BF16),
                vmem((top + rows, chan), F32), vmem((rows, chan), F32), vmem((cycle_len, pad + rows, chan), BF16),
                vmem((stacks, halo_rows, chan), BF16), vmem((stacks + 1, halo_rows, chan), BF16),
                vmem(x.shape, BF16), vmem((rows, chan), BF16),
                vmem((group_n, rows // group_n, chan), F32), vmem((group_n, rows // group_n, chan), F32),
                dma((turns, 4)), dma, dma((batch_n,)), dma((batch_n,)), dma((turns,)), dma((turns,)), dma((2, group_n)), dma((2, group_n)),
            ],
            compiler_params=pltpu.CompilerParams(collective_id=0, has_side_effects=True, vmem_limit_bytes=60 * 2**20),
        )(x, w_cur, w_past, w_res, w_skip)

    return jax.shard_map(local_stack, mesh=mesh, in_specs=(P("dp", "sp", None), P(), P(), P(), P()),
                         out_specs=(P("dp", "sp", None, None), P("dp", "sp", None, None)), check_vma=False)
```

profile of v0, /device:TPU:21, one launch (start us, length us, event | category | flops | bytes accessed | tf_op | source)
XLA Modules:
  0.0 103.7 jit_solution(15906370636800278421)
XLA Ops:
  0.6 99.3 %shard_map.68 = (f32[8,1,128,128]{3,2,1,0:T(8,128)}, f32[8,1,128,128]{3,2,1,0:T(8,128)}) custom-call(bf16[8,128,128]{2,1,0:T(8,128)(2,1)} %x_hbm.1, bf16[16,10,128,256]{3,2,1,0:T(8,128)(2,1)} %wc_hbm.1, bf16[16,10,128,256]{3,2,1,0:T(8,128)(2,1)} %wp_hbm.1, bf16[16,10,128,128]{3,2,1,0:T(8,128)(2,1)} %wr_hbm.1, bf16[16,10,128,128]{3,2,1,0:T(8,128)(2,1)} %ws_hbm.1), custom_call_target="tpu_custom_call" | custom-call | tf_op jit(solution)/shard_map/pallas_call | solution.py:241
  99.9 1.9 %copy.9 = f32[8,1,128,128]{3,2,1,0:T(8,128)} copy(f32[8,1,128,128]{3,2,1,0:T(8,128)} %get-tuple-element.4) | data formatting | bytes 1048576
  101.8 1.9 %copy.10 = f32[8,1,128,128]{3,2,1,0:T(8,128)} copy(f32[8,1,128,128]{3,2,1,0:T(8,128)} %get-tuple-element.5) | data formatting | bytes 1048576
where the time goes:
time: 104 us
  Pallas kernels  99.3 us (95%)
  local copies, waits for them, and re-layouts  3.74 us (4%)
    pallas_call x1, Pallas kernels, local_stack(): pl.pallas_call(functools.partial(kernel, group_n), out_shape=[out, out],...  99.3 us
    unnamed x2, local copies, waits for them, and re-layouts  3.74 us

commit v1 on v0

--- a/solution.py
+++ b/solution.py
@@ -8,8 +8,8 @@
 from jax.sharding import PartitionSpec as P
 
 F32, BF16 = jnp.float32, jnp.bfloat16
-BLOCK = 256
-LAG_GATE, LAG_ADD = 2, 4
+BLOCK = 512
+LAG = 1
 GROUP = 2
 
 
@@ -19,8 +19,8 @@
     return sizes, starts, sum(sizes)
 
 
-def kernel(group_n, x_hbm, wc_hbm, wp_hbm, wr_hbm, ws_hbm, h_out, s_out, w_cur, w_past, w_res, w_skip, h_buf, s_buf, u_buf, halo, tail, x_in, x_all,
-           h_stage, s_stage, w_sem, x_sem, x_send, x_recv, halo_send, halo_recv, out_send, out_recv):
+def kernel(group_n, x_hbm, wc_hbm, wp_hbm, wr_hbm, ws_hbm, both_out, w_cur, w_past, w_res, w_skip, h_buf, s_buf, u_buf, halo, tail, x_in, x_all,
+           stage, w_sem, x_sem, x_send, x_recv, halo_send, halo_recv, out_send, out_recv):
     batch_n, seq_dev, chan = x_in.shape
     stacks, cycle_len = w_cur.shape[:2]
     rows = batch_n * seq_dev
@@ -42,7 +42,7 @@
 
     for turn in range(stacks // GROUP):
         for copy in weight_copies(turn):
-            copy.start()
+            copy.start(priority=1)
 
     barrier = pltpu.get_barrier_semaphore()
     for off in range(1, group_n):
@@ -145,13 +145,12 @@
                 tail[base + part, at:at + last - kept, :] = u[kept - first:]
 
         steps = GROUP * cycle_len * blocks
-        for step in range(steps + LAG_ADD):
-            if step >= LAG_ADD:
-                add(step - LAG_ADD)
-            if LAG_GATE <= step < steps + LAG_GATE:
-                gate(step - LAG_GATE)
+        for step in range(steps + LAG):
             if step < steps:
                 taps(step)
+            if step >= LAG:
+                gate(step - LAG)
+                add(step - LAG)
         pl.when(core < cores - 1)(lambda: halo_copy(turn).start())
         return carry
 
@@ -165,34 +164,29 @@
 
     def out_copies(off, sub):
         target = out_target(off, sub)
-        rank = off * cores + sub
-        found = []
-        for kind, (stage, out) in enumerate(((s_stage, s_out), (h_stage, h_out))):
-            dst = out.at[chip, 0, pl.ds(core * part_rows, part_rows)]
-
-            def local(kind=kind, stage=stage, dst=dst):
-                return pltpu.make_async_copy(stage.at[target], dst, out_recv.at[kind, me])
-
-            def remote(kind=kind, stage=stage, dst=dst):
-                return pltpu.make_async_remote_copy(stage.at[target], dst, out_send.at[kind, rank], out_recv.at[kind, me],
-                                                    device_id={"sp": target}, device_id_type=pl.DeviceIdType.MESH)
-
-            found.append((local, remote))
-        return target, found
+        dst = both_out.at[:, chip, core]
+
+        def remote():
+            return pltpu.make_async_remote_copy(stage.at[target], dst, out_send.at[off * cores + sub], out_recv.at[me],
+                                                device_id={"sp": target}, device_id_type=pl.DeviceIdType.MESH)
+
+        return target, remote
 
     def send(off, sub):
-        target, found = out_copies(off, sub)
-        for local, remote in found:
-            if off:
-                remote().start()
-            else:
-                pl.when(target == me)(lambda: local().start())
-                pl.when(target != me)(lambda: remote().start())
+        target, remote = out_copies(off, sub)
+        if off:
+            remote().start()
+        else:
+            @pl.when(target == me)
+            def _():
+                both_out[:, chip, core] = stage[target]
+
+            pl.when(target != me)(lambda: remote().start())
 
     for rank, (off, sub) in enumerate(spread):
         target = out_target(off, sub)
-        s_stage[target] = s_buf[pl.ds(target, part_rows, stride=group_n), :]
-        h_stage[target] = h_buf[pl.ds(top + target, part_rows, stride=group_n), :]
+        stage[target, 1] = s_buf[pl.ds(target, part_rows, stride=group_n), :]
+        stage[target, 0] = h_buf[pl.ds(top + target, part_rows, stride=group_n), :]
         if rank:
             send(*spread[rank - 1])
     send(*spread[-1])
@@ -213,16 +207,25 @@
         lax.fori_loop(0, stacks // GROUP, end_halo, 0)
 
     for off, sub in spread:
-        target, found = out_copies(off, sub)
-        for local, remote in found:
-            if off:
-                remote().wait_send()
-            else:
-                pl.when(target != me)(lambda: remote().wait_send())
+        target, remote = out_copies(off, sub)
+        if off:
+            remote().wait_send()
+        else:
+            pl.when(target != me)(lambda: remote().wait_send())
     for src in range(group_n):
-        for kind, out in enumerate((s_out, h_out)):
-            dst = out.at[src // cores, 0, pl.ds(src % cores * part_rows, part_rows)]
-            pltpu.make_async_copy(dst, dst, out_recv.at[kind, src]).wait()
+        dst = both_out.at[:, src // cores, src % cores]
+
+        @pl.when(src != me)
+        def _():
+            pltpu.make_async_copy(dst, dst, out_recv.at[src]).wait()
+
+
+def write_out(both, h_out, s_out, sems):
+    copies = [pltpu.make_async_copy(both.at[kind], out, sems.at[kind]) for kind, out in enumerate((h_out, s_out))]
+    for copy in copies:
+        copy.start()
+    for copy in copies:
+        copy.wait()
 
 
 def solution(mesh):
@@ -236,23 +239,27 @@
         pad, top = 2 ** (cycle_len - 1), 8
         turns = stacks // GROUP
         vmem, dma = pltpu.VMEM, pltpu.SemaphoreType.DMA
-        out = jax.ShapeDtypeStruct((batch_n, 1, seq_dev, chan), F32)
-        hbm = pl.BlockSpec(memory_space=pltpu.HBM)
-        return pl.pallas_call(
+        cores, part_rows = group_n // batch_n, rows // group_n
+        hbm, in_vmem = pl.BlockSpec(memory_space=pltpu.HBM), pl.BlockSpec(memory_space=vmem)
+        both = pl.pallas_call(
             functools.partial(kernel, group_n),
-            out_shape=[out, out],
+            out_shape=vmem((2, batch_n, cores, part_rows, chan), F32),
             in_specs=[hbm] * 5,
-            out_specs=[hbm] * 2,
+            out_specs=in_vmem,
             scratch_shapes=[
                 vmem(w_cur.shape, BF16), vmem(w_past.shape, BF16), vmem(w_res.shape, BF16), vmem(w_skip.shape, BF16),
                 vmem((top + rows, chan), F32), vmem((rows, chan), F32), vmem((cycle_len, pad + rows, chan), BF16),
                 vmem((stacks, halo_rows, chan), BF16), vmem((stacks + 1, halo_rows, chan), BF16),
                 vmem(x.shape, BF16), vmem((rows, chan), BF16),
-                vmem((group_n, rows // group_n, chan), F32), vmem((group_n, rows // group_n, chan), F32),
-                dma((turns, 4)), dma, dma((batch_n,)), dma((batch_n,)), dma((turns,)), dma((turns,)), dma((2, group_n)), dma((2, group_n)),
+                vmem((group_n, 2, part_rows, chan), F32),
+                dma((turns, 4)), dma, dma((batch_n,)), dma((batch_n,)), dma((turns,)), dma((turns,)), dma((group_n,)), dma((group_n,)),
             ],
-            compiler_params=pltpu.CompilerParams(collective_id=0, has_side_effects=True, vmem_limit_bytes=60 * 2**20),
-        )(x, w_cur, w_past, w_res, w_skip)
+            compiler_params=pltpu.CompilerParams(collective_id=0, has_side_effects=True, vmem_limit_bytes=50 * 2**20),
+        )(pltpu.with_memory_space_constraint(x, pltpu.HBM), w_cur, w_past, w_res, w_skip)
+        both = pltpu.with_memory_space_constraint(both, pltpu.VMEM)
+        out = jax.ShapeDtypeStruct((batch_n, cores, part_rows, chan), F32)
+        outs = pl.pallas_call(write_out, out_shape=[out, out], in_specs=[in_vmem], out_specs=[hbm] * 2, scratch_shapes=[dma((2,))])(both)
+        return tuple(o.reshape(batch_n, 1, seq_dev, chan) for o in outs)
 
     return jax.shard_map(local_stack, mesh=mesh, in_specs=(P("dp", "sp", None), P(), P(), P(), P()),
                          out_specs=(P("dp", "sp", None, None), P("dp", "sp", None, None)), check_vma=False)

time: 104 us -> 98.4 us (0.946)
  local copies, waits for them, and re-layouts: 3.74 us -> 0 us
  Pallas kernels: 99.3 us -> 97.7 us
    unnamed x2 -> x0, local copies, waits for them, and re-layouts: 3.74 us -> none
    pallas_call x1 -> x2, Pallas kernels: 99.3 us -> 97.7 us  [the longest x1 96.7 us: local_stack(): pl.pallas_call(functools.partial(kernel, group_n), out_shape=vmem((2, bat...]
where the time goes in v1:
time: 98.4 us; the launch traced here: 98.3 us
  Pallas kernels  97.7 us (99%)
    pallas_call x1, Pallas kernels, local_stack(): pl.pallas_call(functools.partial(kernel, group_n), out_shape=vmem((2, bat...  96.7 us

profile of v1, /device:TPU:21, one launch (start us, length us, event | category | flops | bytes accessed | tf_op | source)
XLA Modules:
  0.0 98.3 jit_solution(11826976902389362376)
XLA Ops:
  0.6 96.7 %shard_map.68.both = f32[2,8,2,64,128]{4,3,2,1,0:T(8,128)S(1)} custom-call(bf16[8,128,128]{2,1,0:T(8,128)(2,1)} %x_hbm.1, bf16[16,10,128,256]{3,2,1,0:T(8,128)(2,1)} %wc_hbm.1, bf16[16,10,128,256]{3,2,1,0:T(8,128)(2,1)} %wp_hbm.1, bf16[16,10,128,128]{3,2,1,0:T(8,128)(2,1)} %wr_hbm.1, bf16[16,10,128,128]{3,2,1,0:T(8,128)(2,1)} %ws_hbm.1), custom_call_target="tpu_custom_call" | custom-call | tf_op jit(solution)/shard_map/pallas_call | solution.py:244
  97.3 1.0 %shard_map.69 = (f32[8,2,64,128]{3,2,1,0:T(8,128)}, f32[8,2,64,128]{3,2,1,0:T(8,128)}) custom-call(f32[2,8,2,64,128]{4,3,2,1,0:T(8,128)S(1)} %shard_map.68.both), custom_call_target="tpu_custom_call" | custom-call | tf_op jit(solution)/shard_map/pallas_call | solution.py:261

commit v2 on v1

--- a/solution.py
+++ b/solution.py
@@ -8,8 +8,6 @@
 from jax.sharding import PartitionSpec as P
 
 F32, BF16 = jnp.float32, jnp.bfloat16
-BLOCK = 512
-LAG = 1
 GROUP = 2
 
 
@@ -93,7 +91,6 @@
         return pltpu.make_async_remote_copy(tail.at[part], halo.at[part], halo_send.at[turn], halo_recv.at[turn],
                                             device_id={"sp": jnp.minimum(me + 1, group_n - 1)}, device_id_type=pl.DeviceIdType.MESH)
 
-    blocks = rows // BLOCK
 
     def dot(lhs, rhs):
         return jnp.dot(lhs, rhs, preferred_element_type=F32)
@@ -103,54 +100,28 @@
         for copy in weight_copies(turn):
             copy.wait()
         pl.when(core > 0)(lambda: halo_copy(turn).wait_recv())
-        pre, outs = {}, {}
-
-        def taps(step):
-            layer, block = divmod(step, blocks)
+
+        for layer in range(GROUP * cycle_len):
             part, pos = divmod(layer, cycle_len)
-            dilation = 2**pos
-            if block == 0:
-                got = halo[base + part, starts[pos]:starts[pos] + sizes[pos], :]
+            at, dilation = (base + part, pos), 2**pos
+            got = halo[base + part, starts[pos]:starts[pos] + sizes[pos], :]
+            if dilation == 1:
+                h_buf[0:top, :] = got[sizes[pos] - top:].astype(F32)
+                past = h_buf[top - 1:top + rows - 1, :].astype(BF16)
+            else:
                 u_buf[pos, pad - sizes[pos]:pad, :] = got
-                if pos == 0:
-                    h_buf[0:top, :] = got[sizes[pos] - top:].astype(F32)
-            at = pad + block * BLOCK
-            now = u_buf[pos, at:at + BLOCK, :]
-            if dilation == 1:
-                past = h_buf[top + block * BLOCK - 1:top + (block + 1) * BLOCK - 1, :].astype(BF16)
-            else:
-                past = u_buf[pos, at - dilation:at - dilation + BLOCK, :]
-            both = jnp.concatenate([w_cur[base + part, pos], w_past[base + part, pos]], axis=0)
-            pre[step] = dot(jnp.concatenate([now, past], axis=1), both)
-
-        def gate(step):
-            part, pos = divmod(step // blocks, cycle_len)
-            z = pre.pop(step)
+                past = u_buf[pos, pad - dilation:pad - dilation + rows, :]
+            taps = jnp.concatenate([u_buf[pos, pad:, :], past], axis=1)
+            z = dot(taps, jnp.concatenate([w_cur[at], w_past[at]], axis=0))
             a = (jnp.tanh(z[:, :chan]) * (0.5 * jnp.tanh(0.5 * z[:, chan:]) + 0.5)).astype(BF16)
-            outs[step] = dot(a, jnp.concatenate([w_res[base + part, pos], w_skip[base + part, pos]], axis=1))
-
-        def add(step):
-            layer, block = divmod(step, blocks)
+            out = dot(a, jnp.concatenate([w_res[at], w_skip[at]], axis=1))
+            h = h_buf[top:, :] + out[:, :chan]
+            h_buf[top:, :] = h
+            s_buf[...] = s_buf[...] + out[:, chan:]
+            u = h.astype(BF16)
             part, pos = divmod(layer + 1, cycle_len)
-            out = outs.pop(step)
-            first, last = block * BLOCK, (block + 1) * BLOCK
-            h = h_buf[top + first:top + last, :] + out[:, :chan]
-            h_buf[top + first:top + last, :] = h
-            s_buf[first:last, :] = s_buf[first:last, :] + out[:, chan:]
-            u = h.astype(BF16)
-            u_buf[pos, pad + first:pad + last, :] = u
-            kept = max(first, rows - sizes[pos])
-            if kept < last:
-                at = starts[pos] + kept - (rows - sizes[pos])
-                tail[base + part, at:at + last - kept, :] = u[kept - first:]
-
-        steps = GROUP * cycle_len * blocks
-        for step in range(steps + LAG):
-            if step < steps:
-                taps(step)
-            if step >= LAG:
-                gate(step - LAG)
-                add(step - LAG)
+            u_buf[pos, pad:, :] = u
+            tail[base + part, starts[pos]:starts[pos] + sizes[pos], :] = u[rows - sizes[pos]:]
         pl.when(core < cores - 1)(lambda: halo_copy(turn).start())
         return carry
 

time: 98.4 us -> 93.4 us (0.949)
  Pallas kernels: 97.7 us -> 92.7 us
    pallas_call x1, Pallas kernels: 96.7 us -> 91.7 us  [local_stack(): pl.pallas_call(functools.partial(kernel, group_n), out_shape=vmem((2, bat...]
where the time goes in v2:
time: 93.4 us; the launch traced here: 93.3 us
  Pallas kernels  92.7 us (99%)
    pallas_call x1, Pallas kernels, local_stack(): pl.pallas_call(functools.partial(kernel, group_n), out_shape=vmem((2, bat...  91.7 us

profile of v2, /device:TPU:21, one launch (start us, length us, event | category | flops | bytes accessed | tf_op | source)
XLA Modules:
  0.0 93.3 jit_solution(4015543399523841203)
XLA Ops:
  0.6 91.7 %shard_map.68.both = f32[2,8,2,64,128]{4,3,2,1,0:T(8,128)S(1)} custom-call(bf16[8,128,128]{2,1,0:T(8,128)(2,1)} %x_hbm.1, bf16[16,10,128,256]{3,2,1,0:T(8,128)(2,1)} %wc_hbm.1, bf16[16,10,128,256]{3,2,1,0:T(8,128)(2,1)} %wp_hbm.1, bf16[16,10,128,128]{3,2,1,0:T(8,128)(2,1)} %wr_hbm.1, bf16[16,10,128,128]{3,2,1,0:T(8,128)(2,1)} %ws_hbm.1), custom_call_target="tpu_custom_call" | custom-call | tf_op jit(solution)/shard_map/pallas_call | solution.py:215
  92.3 1.0 %shard_map.69 = (f32[8,2,64,128]{3,2,1,0:T(8,128)}, f32[8,2,64,128]{3,2,1,0:T(8,128)}) custom-call(f32[2,8,2,64,128]{4,3,2,1,0:T(8,128)S(1)} %shard_map.68.both), custom_call_target="tpu_custom_call" | custom-call | tf_op jit(solution)/shard_map/pallas_call | solution.py:232

commit v3 on v2

--- a/solution.py
+++ b/solution.py
@@ -18,7 +18,7 @@
 
 
 def kernel(group_n, x_hbm, wc_hbm, wp_hbm, wr_hbm, ws_hbm, both_out, w_cur, w_past, w_res, w_skip, h_buf, s_buf, u_buf, halo, tail, x_in, x_all,
-           stage, w_sem, x_sem, x_send, x_recv, halo_send, halo_recv, out_send, out_recv):
+           stage, got_out, h_late, u_late, w_sem, x_sem, x_send, x_recv, halo_send, halo_recv, out_send, out_recv):
     batch_n, seq_dev, chan = x_in.shape
     stacks, cycle_len = w_cur.shape[:2]
     rows = batch_n * seq_dev
@@ -95,13 +95,15 @@
     def dot(lhs, rhs):
         return jnp.dot(lhs, rhs, preferred_element_type=F32)
 
-    def group_of_stacks(turn, carry):
+    late = sum(2**pos >= group_n for pos in range(cycle_len))
+
+    def group_of_stacks(turn, layers):
         base = turn * GROUP
         for copy in weight_copies(turn):
             copy.wait()
         pl.when(core > 0)(lambda: halo_copy(turn).wait_recv())
 
-        for layer in range(GROUP * cycle_len):
+        for layer in range(layers):
             part, pos = divmod(layer, cycle_len)
             at, dilation = (base + part, pos), 2**pos
             got = halo[base + part, starts[pos]:starts[pos] + sizes[pos], :]
@@ -123,9 +125,14 @@
             u_buf[pos, pad:, :] = u
             tail[base + part, starts[pos]:starts[pos] + sizes[pos], :] = u[rows - sizes[pos]:]
         pl.when(core < cores - 1)(lambda: halo_copy(turn).start())
+
+    def whole_turn(turn, carry):
+        group_of_stacks(turn, GROUP * cycle_len)
         return carry
 
-    lax.fori_loop(0, stacks // GROUP, group_of_stacks, 0)
+    turns = stacks // GROUP
+    lax.fori_loop(0, turns - 1, whole_turn, 0)
+    group_of_stacks(turns - 1, GROUP * cycle_len - late)
 
     part_rows = rows // group_n
     spread = [(off, sub) for off in far_first for sub in range(cores)]
@@ -133,34 +140,67 @@
     def out_target(off, sub):
         return lax.rem(chip + off, batch_n) * cores + sub
 
-    def out_copies(off, sub):
+    def out_copy(kind, off, sub):
         target = out_target(off, sub)
-        dst = both_out.at[:, chip, core]
-
-        def remote():
-            return pltpu.make_async_remote_copy(stage.at[target], dst, out_send.at[off * cores + sub], out_recv.at[me],
-                                                device_id={"sp": target}, device_id_type=pl.DeviceIdType.MESH)
-
-        return target, remote
-
-    def send(off, sub):
-        target, remote = out_copies(off, sub)
+        return pltpu.make_async_remote_copy(stage.at[kind, target], got_out.at[kind, chip, core], out_send.at[kind, off * cores + sub],
+                                            out_recv.at[kind, me], device_id={"sp": target}, device_id_type=pl.DeviceIdType.MESH)
+
+    def send(kind, off, sub):
         if off:
-            remote().start()
-        else:
+            out_copy(kind, off, sub).start()
+        else:
+            target = out_target(off, sub)
+
             @pl.when(target == me)
             def _():
-                both_out[:, chip, core] = stage[target]
-
-            pl.when(target != me)(lambda: remote().start())
-
-    for rank, (off, sub) in enumerate(spread):
-        target = out_target(off, sub)
-        stage[target, 1] = s_buf[pl.ds(target, part_rows, stride=group_n), :]
-        stage[target, 0] = h_buf[pl.ds(top + target, part_rows, stride=group_n), :]
-        if rank:
-            send(*spread[rank - 1])
-    send(*spread[-1])
+                got_out[kind, chip, core] = stage[kind, target]
+
+            pl.when(target != me)(lambda: out_copy(kind, off, sub).start())
+
+    def receive(kind):
+        for src in range(group_n):
+            dst = got_out.at[kind, src // cores, src % cores]
+
+            @pl.when(src != me)
+            def _():
+                pltpu.make_async_copy(dst, dst, out_recv.at[kind, src]).wait()
+
+    for kind, buf, skipped in ((0, h_buf, top), (1, s_buf, 0)):
+        for rank, (off, sub) in enumerate(spread):
+            target = out_target(off, sub)
+            stage[kind, target] = buf[pl.ds(skipped + target, part_rows, stride=group_n), :]
+            if rank:
+                send(kind, *spread[rank - 1])
+        send(kind, *spread[-1])
+
+    receive(0)
+    pad_late = u_late.shape[1] - seq_dev
+    h = got_out[0].reshape(batch_n, seq_dev, chan)
+    h_late[:, 0:top, :] = jnp.zeros((batch_n, top, chan), F32)
+    h_late[:, top:, :] = h
+    u_late[:, 0:pad_late, :] = jnp.zeros((batch_n, pad_late, chan), BF16)
+    u_late[:, pad_late:, :] = h.astype(BF16)
+    for pos in range(cycle_len - late, cycle_len):
+        at, shift = (stacks - 1, pos), 2**pos // group_n
+        if shift == 1:
+            past = h_late[:, top - 1:top + seq_dev - 1, :].astype(BF16)
+        else:
+            past = u_late[:, pad_late - shift:pad_late - shift + seq_dev, :]
+        taps = jnp.concatenate([u_late[:, pad_late:, :], past], axis=2).reshape(rows, 2 * chan)
+        z = dot(taps, jnp.concatenate([w_cur[at], w_past[at]], axis=0))
+        a = (jnp.tanh(z[:, :chan]) * (0.5 * jnp.tanh(0.5 * z[:, chan:]) + 0.5)).astype(BF16)
+        out = dot(a, jnp.concatenate([w_res[at], w_skip[at]], axis=1)).reshape(batch_n, seq_dev, 2 * chan)
+        h = h_late[:, top:, :] + out[:, :, :chan]
+        h_late[:, top:, :] = h
+        u_late[:, pad_late:, :] = h.astype(BF16)
+        more = out[:, :, chan:]
+        if pos == cycle_len - late:
+            both_out[1] = more
+        else:
+            both_out[1] = both_out[1] + more
+    both_out[0] = h_late[:, top:, :]
+    receive(1)
+    both_out[1] = got_out[1].reshape(batch_n, seq_dev, chan) + both_out[1]
 
     for off in range(batch_n):
         target, local, remote = x_copies(off)
@@ -177,18 +217,12 @@
     def _():
         lax.fori_loop(0, stacks // GROUP, end_halo, 0)
 
-    for off, sub in spread:
-        target, remote = out_copies(off, sub)
-        if off:
-            remote().wait_send()
-        else:
-            pl.when(target != me)(lambda: remote().wait_send())
-    for src in range(group_n):
-        dst = both_out.at[:, src // cores, src % cores]
-
-        @pl.when(src != me)
-        def _():
-            pltpu.make_async_copy(dst, dst, out_recv.at[src]).wait()
+    for kind in range(2):
+        for off, sub in spread:
+            if off:
+                out_copy(kind, off, sub).wait_send()
+            else:
+                pl.when(out_target(off, sub) != me)(lambda: out_copy(kind, off, sub).wait_send())
 
 
 def write_out(both, h_out, s_out, sems):
@@ -208,13 +242,14 @@
         rows = batch_n * seq_dev
         sizes, starts, halo_rows = halo_slots(cycle_len)
         pad, top = 2 ** (cycle_len - 1), 8
+        pad_late = max(16, pad // group_n)
         turns = stacks // GROUP
         vmem, dma = pltpu.VMEM, pltpu.SemaphoreType.DMA
         cores, part_rows = group_n // batch_n, rows // group_n
         hbm, in_vmem = pl.BlockSpec(memory_space=pltpu.HBM), pl.BlockSpec(memory_space=vmem)
         both = pl.pallas_call(
             functools.partial(kernel, group_n),
-            out_shape=vmem((2, batch_n, cores, part_rows, chan), F32),
+            out_shape=vmem((2,) + x.shape, F32),
             in_specs=[hbm] * 5,
             out_specs=in_vmem,
             scratch_shapes=[
@@ -222,13 +257,14 @@
                 vmem((top + rows, chan), F32), vmem((rows, chan), F32), vmem((cycle_len, pad + rows, chan), BF16),
                 vmem((stacks, halo_rows, chan), BF16), vmem((stacks + 1, halo_rows, chan), BF16),
                 vmem(x.shape, BF16), vmem((rows, chan), BF16),
-                vmem((group_n, 2, part_rows, chan), F32),
-                dma((turns, 4)), dma, dma((batch_n,)), dma((batch_n,)), dma((turns,)), dma((turns,)), dma((group_n,)), dma((group_n,)),
+                vmem((2, group_n, part_rows, chan), F32), vmem((2, batch_n, cores, part_rows, chan), F32),
+                vmem((batch_n, top + seq_dev, chan), F32), vmem((batch_n, pad_late + seq_dev, chan), BF16),
+                dma((turns, 4)), dma, dma((batch_n,)), dma((batch_n,)), dma((turns,)), dma((turns,)), dma((2, group_n)), dma((2, group_n)),
             ],
-            compiler_params=pltpu.CompilerParams(collective_id=0, has_side_effects=True, vmem_limit_bytes=50 * 2**20),
+            compiler_params=pltpu.CompilerParams(collective_id=0, has_side_effects=True, vmem_limit_bytes=52 * 2**20),
         )(pltpu.with_memory_space_constraint(x, pltpu.HBM), w_cur, w_past, w_res, w_skip)
         both = pltpu.with_memory_space_constraint(both, pltpu.VMEM)
-        out = jax.ShapeDtypeStruct((batch_n, cores, part_rows, chan), F32)
+        out = jax.ShapeDtypeStruct(x.shape, F32)
         outs = pl.pallas_call(write_out, out_shape=[out, out], in_specs=[in_vmem], out_specs=[hbm] * 2, scratch_shapes=[dma((2,))])(both)
         return tuple(o.reshape(batch_n, 1, seq_dev, chan) for o in outs)
 

time: 93.4 us -> 92.1 us (0.986)
  Pallas kernels: 92.7 us -> 91.2 us
    pallas_call x1, Pallas kernels: 91.7 us -> 90.2 us  [local_stack(): pl.pallas_call(functools.partial(kernel, group_n), out_shape=vmem((2,) +...]
where the time goes in v3:
time: 92.1 us; the launch traced here: 92 us
  Pallas kernels  91.2 us (99%)
    pallas_call x1, Pallas kernels, local_stack(): pl.pallas_call(functools.partial(kernel, group_n), out_shape=vmem((2,) +...  90.2 us

profile of v3, /device:TPU:21, one launch (start us, length us, event | category | flops | bytes accessed | tf_op | source)
XLA Modules:
  0.0 92.0 jit_solution(10181903160143415067)
XLA Ops:
  0.6 90.2 %shard_map.68.both = f32[2,8,128,128]{3,2,1,0:T(8,128)S(1)} custom-call(bf16[8,128,128]{2,1,0:T(8,128)(2,1)} %x_hbm.1, bf16[16,10,128,256]{3,2,1,0:T(8,128)(2,1)} %wc_hbm.1, bf16[16,10,128,256]{3,2,1,0:T(8,128)(2,1)} %wp_hbm.1, bf16[16,10,128,128]{3,2,1,0:T(8,128)(2,1)} %wr_hbm.1, bf16[16,10,128,128]{3,2,1,0:T(8,128)(2,1)} %ws_hbm.1), custom_call_target="tpu_custom_call" | custom-call | tf_op jit(solution)/shard_map/pallas_call | solution.py:250
  90.8 1.0 %shard_map.69 = (f32[8,128,128]{2,1,0:T(8,128)}, f32[8,128,128]{2,1,0:T(8,128)}) custom-call(f32[2,8,128,128]{3,2,1,0:T(8,128)S(1)} %shard_map.68.both), custom_call_target="tpu_custom_call" | custom-call | tf_op jit(solution)/shard_map/pallas_call | solution.py:268

commit v4 on v3

--- a/solution.py
+++ b/solution.py
@@ -9,6 +9,7 @@
 
 F32, BF16 = jnp.float32, jnp.bfloat16
 GROUP = 2
+UNROLL = 2
 
 
 def halo_slots(cycle_len):
@@ -126,13 +127,17 @@
             tail[base + part, starts[pos]:starts[pos] + sizes[pos], :] = u[rows - sizes[pos]:]
         pl.when(core < cores - 1)(lambda: halo_copy(turn).start())
 
-    def whole_turn(turn, carry):
-        group_of_stacks(turn, GROUP * cycle_len)
+    turns = stacks // GROUP
+
+    def body(trip, carry):
+        for k in range(UNROLL):
+            group_of_stacks(trip * UNROLL + k, GROUP * cycle_len)
         return carry
 
-    turns = stacks // GROUP
-    lax.fori_loop(0, turns - 1, whole_turn, 0)
-    group_of_stacks(turns - 1, GROUP * cycle_len - late)
+    trips = (turns - 1) // UNROLL
+    lax.fori_loop(0, trips, body, 0)
+    for turn in range(trips * UNROLL, turns):
+        group_of_stacks(turn, GROUP * cycle_len - (late if turn == turns - 1 else 0))
 
     part_rows = rows // group_n
     spread = [(off, sub) for off in far_first for sub in range(cores)]

time: 92.1 us -> 91.7 us (level)
  no operation moved by 1% of the time
where the time goes in v4:
time: 91.7 us; the launch traced here: 91.6 us
  Pallas kernels  90.8 us (99%)
    pallas_call x1, Pallas kernels, local_stack(): pl.pallas_call(functools.partial(kernel, group_n), out_shape=vmem((2,) +...  89.8 us

profile of v4, /device:TPU:21, one launch (start us, length us, event | category | flops | bytes accessed | tf_op | source)
XLA Modules:
  0.0 91.6 jit_solution(6145696861974876177)
XLA Ops:
  0.6 89.8 %shard_map.68.both = f32[2,8,128,128]{3,2,1,0:T(8,128)S(1)} custom-call(bf16[8,128,128]{2,1,0:T(8,128)(2,1)} %x_hbm.1, bf16[16,10,128,256]{3,2,1,0:T(8,128)(2,1)} %wc_hbm.1, bf16[16,10,128,256]{3,2,1,0:T(8,128)(2,1)} %wp_hbm.1, bf16[16,10,128,128]{3,2,1,0:T(8,128)(2,1)} %wr_hbm.1, bf16[16,10,128,128]{3,2,1,0:T(8,128)(2,1)} %ws_hbm.1), custom_call_target="tpu_custom_call" | custom-call | tf_op jit(solution)/shard_map/pallas_call | solution.py:255
  90.5 1.0 %shard_map.69 = (f32[8,128,128]{2,1,0:T(8,128)}, f32[8,128,128]{2,1,0:T(8,128)}) custom-call(f32[2,8,128,128]{3,2,1,0:T(8,128)S(1)} %shard_map.68.both), custom_call_target="tpu_custom_call" | custom-call | tf_op jit(solution)/shard_map/pallas_call | solution.py:273

commit v5 on v4

--- a/solution.py
+++ b/solution.py
@@ -204,9 +204,6 @@
         else:
             both_out[1] = both_out[1] + more
     both_out[0] = h_late[:, top:, :]
-    receive(1)
-    both_out[1] = got_out[1].reshape(batch_n, seq_dev, chan) + both_out[1]
-
     for off in range(batch_n):
         target, local, remote = x_copies(off)
         if off:
@@ -228,6 +225,9 @@
                 out_copy(kind, off, sub).wait_send()
             else:
                 pl.when(out_target(off, sub) != me)(lambda: out_copy(kind, off, sub).wait_send())
+
+    receive(1)
+    both_out[1] = got_out[1].reshape(batch_n, seq_dev, chan) + both_out[1]
 
 
 def write_out(both, h_out, s_out, sems):

time: 91.7 us -> 91.7 us (level)
  no operation moved by 1% of the time
where the time goes in v5:
time: 91.7 us; the launch traced here: 91.6 us
  Pallas kernels  90.8 us (99%)
    pallas_call x1, Pallas kernels, local_stack(): pl.pallas_call(functools.partial(kernel, group_n), out_shape=vmem((2,) +...  89.8 us

profile of v5, /device:TPU:21, one launch (start us, length us, event | category | flops | bytes accessed | tf_op | source)
XLA Modules:
  0.0 91.6 jit_solution(14895466402734924742)
XLA Ops:
  0.6 89.8 %shard_map.68.both = f32[2,8,128,128]{3,2,1,0:T(8,128)S(1)} custom-call(bf16[8,128,128]{2,1,0:T(8,128)(2,1)} %x_hbm.1, bf16[16,10,128,256]{3,2,1,0:T(8,128)(2,1)} %wc_hbm.1, bf16[16,10,128,256]{3,2,1,0:T(8,128)(2,1)} %wp_hbm.1, bf16[16,10,128,128]{3,2,1,0:T(8,128)(2,1)} %wr_hbm.1, bf16[16,10,128,128]{3,2,1,0:T(8,128)(2,1)} %ws_hbm.1), custom_call_target="tpu_custom_call" | custom-call | tf_op jit(solution)/shard_map/pallas_call | solution.py:255
  90.4 1.0 %shard_map.69 = (f32[8,128,128]{2,1,0:T(8,128)}, f32[8,128,128]{2,1,0:T(8,128)}) custom-call(f32[2,8,128,128]{3,2,1,0:T(8,128)S(1)} %shard_map.68.both), custom_call_target="tpu_custom_call" | custom-call | tf_op jit(solution)/shard_map/pallas_call | solution.py:273
